TPU v7x, 32 devices: a whole 2x2x4 slice. The times are simulated.
32 devices in a mesh: patch: 16 (over z, y, x), width: 2 (over core).
Axes of the slice: x: 2, y: 2, z: 4, core: 2. Of those that a mesh axis runs over, the one named last changes fastest.
Arguments:
- node_latents: bfloat16 [512, 2048], P('width', 'patch'), may hold values from -6 to 6
- edge_latents: bfloat16 [512, 16384], P('width', 'patch'), may hold values from -6 to 6
- senders: int32 [16384], P('patch'), may hold values from 0 to 2047, as said below
- receivers: int32 [16384], P('patch'), may hold values from 0 to 2047, as said below
- edge_count: int32 [16], P('patch'), may hold values from 512 to 1024, as said below
- edge_in_weight: bfloat16 [2, 512, 1536], P(None, 'width'), may hold values from -0.15625 to 0.15625
- edge_in_bias: float32 [2, 512], P(None, 'width'), may hold values from -3 to 3
- edge_out_weight: bfloat16 [2, 512, 512], P(None, 'width'), may hold values from -0.25 to 0.25
- edge_out_bias: float32 [2, 512], P(None, 'width'), may hold values from -3 to 3
- edge_gain: float32 [2, 512], P(None, 'width'), may hold values from 0.1 to 1.9
- edge_shift: float32 [2, 512], P(None, 'width'), may hold values from -3 to 3
- node_in_weight: bfloat16 [2, 512, 1024], P(None, 'width'), may hold values from -0.1875 to 0.1875
- node_in_bias: float32 [2, 512], P(None, 'width'), may hold values from -3 to 3
- node_out_weight: bfloat16 [2, 512, 512], P(None, 'width'), may hold values from -0.25 to 0.25
- node_out_bias: float32 [2, 512], P(None, 'width'), may hold values from -3 to 3
- node_gain: float32 [2, 512], P(None, 'width'), may hold values from 0.1 to 1.9
- node_shift: float32 [2, 512], P(None, 'width'), may hold values from -3 to 3
Outputs:
- nodes_out: bfloat16 [512, 2048], P('width', 'patch')
- edges_out: bfloat16 [512, 16384], P('width', 'patch')
Inputs may be any that keep to these rules, and one draw needn't show every extreme that they name: `senders`: the sender of a slot of patch p is a node of patch p, of patch p - 1 or p + 1 (counted around, modulo the number of patches), or one of the first 16 nodes of some patch. `receivers`: row r names a node of patch r // 1024, from (r // 1024) * 128 to that plus 128 - 1. Slots p * 1024 to p * 1024 + edge_count[p] - 1 of patch p are live, the rest are padding; some patch has all 1024 slots live.
All inputs are finite; a program needn't handle non-finite values.
Results may differ from a plain program's by a relative error of at most 0.014.
Values may be sent and summed in bfloat16 or wider, within the bound.
A program may use at most 64 MiB of HBM per device.

v0:
```python
import jax
import jax.numpy as jnp
from jax import lax
from jax.sharding import PartitionSpec as P

epsilon = 1e-05


def with_halo(shard, sides, width):
    for axis, dim in sides:
        size, length = (lax.axis_size(axis), shard.shape[dim])
        up = [(i, (i + 1) % size) for i in range(size)]
        down = [(j, i) for i, j in up]
        last = lax.slice_in_dim(shard, length - width, length, axis=dim)
        initial = lax.slice_in_dim(shard, 0, width, axis=dim)
        before = lax.ppermute(last, axis, up)
        after = lax.ppermute(initial, axis, down)
        shard = jnp.concatenate([before, shard, after], axis=dim)
    return shard


def normalize(values, totals, gain, shift, model_width):
    mean = totals[0][None, :] / model_width
    square = totals[1][None, :] / model_width
    return (values - mean) * lax.rsqrt(square - mean * mean + epsilon) * gain[:, None] + shift[
        :, None
    ]


def contract_first(left, right):
    return lax.dot_general(
        left, right, (((0,), (0,)), ((), ())), preferred_element_type=jnp.float32
    )


def on_device(
    node_latents,
    edge_latents,
    senders,
    receivers,
    edge_count,
    edge_in_weight,
    edge_in_bias,
    edge_out_weight,
    edge_out_bias,
    edge_gain,
    edge_shift,
    node_in_weight,
    node_in_bias,
    node_out_weight,
    node_out_bias,
    node_gain,
    node_shift,
):
    width_part, node_rows = node_latents.shape
    edge_rows = edge_latents.shape[1]
    model_width = edge_out_weight.shape[2]
    layers = edge_in_weight.shape[0]
    coarse_rows = node_rows // 8
    patch_here = lax.axis_index("patch")
    patch_start = patch_here * node_rows
    local_receiver = receivers - patch_start
    live = jnp.arange(edge_rows, dtype=jnp.int32) < edge_count[0]
    incidence = (
        (local_receiver[None, :] == jnp.arange(node_rows, dtype=jnp.int32)[:, None]) & live[None, :]
    ).astype(jnp.bfloat16)
    patch_count = lax.axis_size("patch")
    owner_patch = senders // node_rows
    within = senders - owner_patch * node_rows
    below = (patch_here + patch_count - 1) % patch_count
    above = (patch_here + 1) % patch_count
    far_index = 3 * node_rows + owner_patch * coarse_rows + within
    sender_index = jnp.where(
        owner_patch == patch_here,
        node_rows + within,
        jnp.where(
            owner_patch == below,
            within,
            jnp.where(owner_patch == above, 2 * node_rows + within, far_index),
        ),
    )
    nodes = node_latents
    edges = edge_latents
    for layer in range(layers):
        w_edge = edge_in_weight[layer]
        w_node = node_in_weight[layer]
        piece = lax.all_gather(nodes, "width", axis=0, tiled=True)
        count = piece.shape[0]

        def product(offset, weight):
            columns = lax.dynamic_slice_in_dim(weight, offset, count, 1)
            return jnp.dot(columns, piece, preferred_element_type=jnp.float32)

        sender_sum = product(model_width, w_edge)
        receiver_sum = product(2 * model_width, w_edge)
        node_first = product(0, w_node)
        sender_part = sender_sum.astype(jnp.bfloat16)
        receiver_part = receiver_sum.astype(jnp.bfloat16)
        beside_all = with_halo(sender_part, (("patch", 1),), node_rows)
        coarse = lax.all_gather(sender_part[:, :coarse_rows], "patch", axis=1, tiled=True)
        table = jnp.concatenate([beside_all, coarse], axis=1)
        edge_piece = lax.all_gather(edges, "width", axis=0, tiled=True)
        edge_columns = lax.slice_in_dim(w_edge, 0, edge_piece.shape[0], axis=1)
        edge_first = jnp.dot(edge_columns, edge_piece, preferred_element_type=jnp.float32)
        before = edge_first + jnp.take(table, sender_index, axis=1).astype(jnp.float32)
        before = (
            before
            + jnp.take(receiver_part, local_receiver, axis=1).astype(jnp.float32)
            + edge_in_bias[layer][:, None]
        )
        edge_hidden = jax.nn.silu(before).astype(jnp.bfloat16)
        edge_rows_weight = edge_out_weight[layer]
        edge_partial = contract_first(edge_rows_weight, edge_hidden)
        edge_mlp = lax.psum_scatter(
            edge_partial.astype(jnp.bfloat16), "width", scatter_dimension=0, tiled=True
        ).astype(jnp.float32)
        edge_mlp = edge_mlp + edge_out_bias[layer][:, None]
        edge_totals = lax.psum(
            (jnp.sum(edge_mlp, axis=0), jnp.sum(edge_mlp * edge_mlp, axis=0)), "width"
        )
        updated = edges.astype(jnp.float32) + normalize(
            edge_mlp, edge_totals, edge_gain[layer], edge_shift[layer], model_width
        )
        edges = jnp.where(live[None, :], updated, jnp.float32(0.0)).astype(jnp.bfloat16)
        aggregate = lax.dot_general(
            edges, incidence, (((1,), (1,)), ((), ())), preferred_element_type=jnp.float32
        ).astype(jnp.bfloat16)
        aggregate_piece = lax.all_gather(aggregate, "width", axis=0, tiled=True)
        aggregate_columns = lax.dynamic_slice_in_dim(
            w_node, model_width, aggregate_piece.shape[0], 1
        )
        node_second = jnp.dot(
            aggregate_columns, aggregate_piece, preferred_element_type=jnp.float32
        )
        node_hidden = jax.nn.silu(node_first + node_second + node_in_bias[layer][:, None]).astype(
            jnp.bfloat16
        )
        node_rows_weight = node_out_weight[layer]
        node_partial = contract_first(node_rows_weight, node_hidden)
        node_mlp = lax.psum_scatter(
            node_partial.astype(jnp.bfloat16), "width", scatter_dimension=0, tiled=True
        ).astype(jnp.float32)
        node_mlp = node_mlp + node_out_bias[layer][:, None]
        node_totals = lax.psum(
            (jnp.sum(node_mlp, axis=0), jnp.sum(node_mlp * node_mlp, axis=0)), "width"
        )
        nodes = (
            nodes.astype(jnp.float32)
            + normalize(node_mlp, node_totals, node_gain[layer], node_shift[layer], model_width)
        ).astype(jnp.bfloat16)
    return (nodes, edges)


def solution(mesh):
    return jax.shard_map(
        on_device,
        mesh=mesh,
        in_specs=(
            P("width", "patch"),
            P("width", "patch"),
            P("patch"),
            P("patch"),
            P("patch"),
            P(None, "width", None),
            P(None, "width"),
            P(None, "width", None),
            P(None, "width"),
            P(None, "width"),
            P(None, "width"),
            P(None, "width", None),
            P(None, "width"),
            P(None, "width", None),
            P(None, "width"),
            P(None, "width"),
            P(None, "width"),
        ),
        out_specs=(P("width", "patch"), P("width", "patch")),
        check_vma=False,
    )
```

profile of v0, /device:TPU:0, one launch (start us, length us, event | category | flops | bytes accessed | tf_op | source)
XLA Modules:
  0.0 188.5 jit_solution(8315396250891950671)
XLA Ops:
  8.7 2.0 %all_gather.24 = bf16[512,128]{1,0:T(8,128)(2,1)S(1)} all-gather(bf16[256,128]{1,0:T(8,128)(2,1)S(1)} %copy-done.3), channel_id=1, replica_groups=mesh['patch'=16,'width'=2] {'width'}, dimensions={0}, use_global_device_ids=true | all-gather | bytes 196608 | tf_op jit(solution)/shard_map/all_gather | solution.py:87
  11.0 2.9 %collective-permute-start = (bf16[256,128]{0,1:T(8,128)(2,1)S(1)}, bf16[256,128]{0,1:T(8,128)(2,1)S(1)}, u32[]{:S(2)}, u32[]{:S(2)}) collective-permute-start(bf16[256,128]{0,1:T(8,128)(2,1)S(1)} %convolution_convert_fusion.9), channel_id=1, source_target_pairs={{0,2},{2,4},{4,6},{6,8},{8,10},{10,12},{12,14},{14,16},{16,18},{18... | collective-permute-start | bytes 196616 | tf_op jit(solution)/shard_map/ppermute | solution.py:16
  13.9 4.1 %collective-permute-start.1 = (bf16[256,128]{0,1:T(8,128)(2,1)S(1)}, bf16[256,128]{0,1:T(8,128)(2,1)S(1)}, u32[]{:S(2)}, u32[]{:S(2)}) collective-permute-start(bf16[256,128]{0,1:T(8,128)(2,1)S(1)} %convolution_convert_fusion.9), channel_id=1, source_target_pairs={{2,0},{4,2},{6,4},{8,6},{10,8},{12,10},{14,12},{16,14},{18,16},{20... | collective-permute-start | bytes 196616 | tf_op jit(solution)/shard_map/ppermute | solution.py:17
  18.5 3.9 %gather_fusion.1 = bf16[1024,256]{1,0:T(8,128)(2,1)S(1)} fusion(bf16[256,128]{0,1:T(8,128)(2,1)S(1)} %copy.22, s32[1024]{0:T(1024)S(1)} %fusion.84), kind=kCustom, calls=%fused_computation.1.clone | custom fusion | bytes 1052672 | tf_op jit(solution)/shard_map/jit(_take)/gather | solution.py:108
  22.6 38.1 %all_gather.26 = bf16[256,256]{0,1:T(8,128)(2,1)S(1)} all-gather(bf16[256,16]{0,1:T(8,128)(2,1)S(1)} %slice.121), channel_id=1, replica_groups=mesh['patch'=16,'width'=2] {'patch'}, dimensions={1}, use_global_device_ids=true | all-gather | bytes 139264 | tf_op jit(solution)/shard_map/all_gather | solution.py:100
  60.8 3.9 %gather_fusion = bf16[1024,256]{1,0:T(8,128)(2,1)S(1)} fusion(bf16[256,640]{0,1:T(8,128)(2,1)S(1)} %pad_maximum_fusion, s32[1024]{0:T(1024)S(1)} %broadcast_clamp_fusion), kind=kCustom, calls=%fused_computation.clone | custom fusion | bytes 1052672 | tf_op jit(solution)/shard_map/jit(_take)/gather | solution.py:105
  65.0 3.3 %fusion = bf16[512,1024]{0,1:T(8,128)(2,1)} fusion(bf16[512,1024]{1,0:T(8,128)(2,1)} %all-gather.3.cloned.1.call-done, bf16[1024,256]{0,1:T(8,128)(2,1)S(1)} %copy.23, bf16[1024,256]{0,1:T(8,128)(2,1)S(1)} %copy.21, f32[256]{0:T(256)S(1)} %bitcast.129, pred[1024]{0:T(1024)(128)(4,1)S(1)} %get-tuple-element.24, pred[1024]{0:T(1024)(128)(4,1)S(1)} %get-tuple-element.54, ...), kind=kOutput, calls=%fused_computation.6 | convolution fusion | flops 540540928 | bytes 3673088 | tf_op jit(solution)/shard_map/dot_general | solution.py:31
  74.1 2.5 %all-reduce.3 = (f32[1024]{0:T(1024)S(1)}, f32[1024]{0:T(1024)S(1)}) all-reduce(f32[1024]{0:T(1024)S(1)} %get-tuple-element.9, f32[1024]{0:T(1024)S(1)} %get-tuple-element.8), channel_id=1, replica_groups=mesh['patch'=16,'width'=2] {'width'}, use_global_device_ids=true, to_apply=%region_4.7 | all-reduce | flops 2048 | bytes 16384 | tf_op jit(solution)/shard_map/psum | solution.py:118
  78.9 1.9 %all_gather.27 = bf16[512,128]{1,0:T(8,128)(2,1)S(1)} all-gather(bf16[256,128]{1,0:T(8,128)(2,1)S(1)} %convolution_convert_fusion.7), channel_id=1, replica_groups=mesh['patch'=16,'width'=2] {'width'}, dimensions={0}, use_global_device_ids=true | all-gather | bytes 196608 | tf_op jit(solution)/shard_map/all_gather | solution.py:128
  80.8 2.0 %fusion.11 = bf16[512,128]{0,1:T(8,128)(2,1)} fusion(bf16[2,256,512]{2,1,0:T(8,128)(2,1)} %param.34, f32[256,128]{1,0:T(8,128)S(1)} %fusion.52, bf16[512,128]{1,0:T(8,128)(2,1)S(1)} %all_gather.27, bf16[256,1024]{1,0:T(8,128)(2,1)S(1)} %get-tuple-element.29, f32[256]{0:T(256)S(1)} %bitcast.128), kind=kOutput, calls=%fused_computation.23 | convolution fusion | flops 67403776 | bytes 918528 | tf_op jit(solution)/shard_map/dot_general | solution.py:31
  83.5 8.3 %reduce-scatter.7.cloned.1.call-done = bf16[256,128]{0,1:T(8,128)(2,1)} async-done(((bf16[512,128]{0,1:T(8,128)(2,1)}), bf16[256,128]{0,1:T(8,128)(2,1)}) %reduce-scatter.7.cloned.1.call-update) | async-done | bytes 65552 | tf_op jit(solution)/shard_map/reduce_scatter | solution.py:140
  92.7 2.5 %all-reduce.2 = (f32[128]{0:T(128)S(1)}, f32[128]{0:T(128)S(1)}) all-reduce(f32[128]{0:T(128)S(1)} %get-tuple-element.13, f32[128]{0:T(128)S(1)} %get-tuple-element.12), channel_id=1, replica_groups=mesh['patch'=16,'width'=2] {'width'}, use_global_device_ids=true, to_apply=%region_9.12 | all-reduce | flops 256 | bytes 2048 | tf_op jit(solution)/shard_map/psum | solution.py:144
  96.1 1.9 %all_gather.28 = bf16[512,128]{0,1:T(8,128)(2,1)S(1)} all-gather(bf16[256,128]{0,1:T(8,128)(2,1)S(1)} %add_convert_fusion.1), channel_id=1, replica_groups=mesh['patch'=16,'width'=2] {'width'}, dimensions={0}, use_global_device_ids=true | all-gather | bytes 196608 | tf_op jit(solution)/shard_map/all_gather | solution.py:87
  100.0 3.9 %collective-permute-start.3 = (bf16[256,128]{0,1:T(8,128)(2,1)S(1)}, bf16[256,128]{0,1:T(8,128)(2,1)S(1)}, u32[]{:S(2)}, u32[]{:S(2)}) collective-permute-start(bf16[256,128]{0,1:T(8,128)(2,1)S(1)} %fusion.13), channel_id=1, source_target_pairs={{2,0},{4,2},{6,4},{8,6},{10,8},{12,10},{14,12},{16,14},{18,16},{20... | collective-permute-start | bytes 196616 | tf_op jit(solution)/shard_map/ppermute | solution.py:17
  104.2 3.9 %gather_fusion.3 = bf16[1024,256]{1,0:T(8,128)(2,1)S(1)} fusion(bf16[256,128]{0,1:T(8,128)(2,1)S(1)} %fusion.14, s32[1024]{0:T(1024)S(1)} %fusion.84), kind=kCustom, calls=%fused_computation.3.clone | custom fusion | bytes 1052672 | tf_op jit(solution)/shard_map/jit(_take)/gather | solution.py:108
  108.3 37.9 %all_gather.30 = bf16[256,256]{0,1:T(8,128)(2,1)S(1)} all-gather(bf16[256,16]{0,1:T(8,128)(2,1)S(1)} %slice.123), channel_id=1, replica_groups=mesh['patch'=16,'width'=2] {'patch'}, dimensions={1}, use_global_device_ids=true | all-gather | bytes 139264 | tf_op jit(solution)/shard_map/all_gather | solution.py:100
  146.3 3.9 %gather_fusion.2 = bf16[1024,256]{1,0:T(8,128)(2,1)S(1)} fusion(bf16[256,640]{0,1:T(8,128)(2,1)S(1)} %pad_maximum_fusion.1, s32[1024]{0:T(1024)S(1)} %broadcast_clamp_fusion), kind=kCustom, calls=%fused_computation.2.clone | custom fusion | bytes 1052672 | tf_op jit(solution)/shard_map/jit(_take)/gather | solution.py:105
  150.5 3.3 %fusion.1 = bf16[512,1024]{0,1:T(8,128)(2,1)} fusion(bf16[512,1024]{0,1:T(8,128)(2,1)} %all-gather.5.cloned.1.call-done, bf16[1024,256]{0,1:T(8,128)(2,1)S(1)} %copy.27, bf16[1024,256]{0,1:T(8,128)(2,1)S(1)} %copy.26, f32[256]{0:T(256)S(1)} %bitcast.126, pred[1024]{0:T(1024)(128)(4,1)S(1)} %get-tuple-element.24, pred[1024]{0:T(1024)(128)(4,1)S(1)} %get-tuple-element.54, ...), kind=kOutput, calls=%fused_computation.7 | convolution fusion | flops 540540928 | bytes 3673088 | tf_op jit(solution)/shard_map/dot_general | solution.py:31
  154.1 4.3 %reduce-scatter.9.cloned.1.call-done = bf16[256,1024]{0,1:T(8,128)(2,1)} async-done(((bf16[512,1024]{0,1:T(8,128)(2,1)}), bf16[256,1024]{0,1:T(8,128)(2,1)}) %reduce-scatter.9.cloned.1.call-update) | async-done | bytes 524304 | tf_op jit(solution)/shard_map/reduce_scatter | solution.py:114
  159.9 2.5 %all-reduce.1 = (f32[1024]{0:T(1024)S(1)}, f32[1024]{0:T(1024)S(1)}) all-reduce(f32[1024]{0:T(1024)S(1)} %get-tuple-element.7, f32[1024]{0:T(1024)S(1)} %get-tuple-element.6), channel_id=1, replica_groups=mesh['patch'=16,'width'=2] {'width'}, use_global_device_ids=true, to_apply=%region_14.17 | all-reduce | flops 2048 | bytes 16384 | tf_op jit(solution)/shard_map/psum | solution.py:118
  162.4 1.9 select_convert_fusion
  164.6 1.9 %all_gather.31 = bf16[512,128]{1,0:T(8,128)(2,1)S(1)} all-gather(bf16[256,128]{1,0:T(8,128)(2,1)S(1)} %convolution_convert_fusion.4), channel_id=1, replica_groups=mesh['patch'=16,'width'=2] {'width'}, dimensions={0}, use_global_device_ids=true | all-gather | bytes 196608 | tf_op jit(solution)/shard_map/all_gather | solution.py:128
  168.6 7.9 %reduce-scatter.11.cloned.1.call-done = bf16[256,128]{0,1:T(8,128)(2,1)} async-done(((bf16[512,128]{0,1:T(8,128)(2,1)}), bf16[256,128]{0,1:T(8,128)(2,1)}) %reduce-scatter.11.cloned.1.call-update) | async-done | bytes 65552 | tf_op jit(solution)/shard_map/reduce_scatter | solution.py:140
  177.5 2.5 %all-reduce = (f32[128]{0:T(128)S(1)}, f32[128]{0:T(128)S(1)}) all-reduce(f32[128]{0:T(128)S(1)} %get-tuple-element.11, f32[128]{0:T(128)S(1)} %get-tuple-element.10), channel_id=1, replica_groups=mesh['patch'=16,'width'=2] {'width'}, use_global_device_ids=true, to_apply=%region_19.22 | all-reduce | flops 256 | bytes 2048 | tf_op jit(solution)/shard_map/psum | solution.py:144
  (97 shorter events, 21.9 us)
Async XLA Ops:
  7.2 1.6 copy-start.3
  7.2 10.9 %copy-start.5 = (s32[1024]{0:T(1024)S(1)}, s32[1024]{0:T(1024)}, u32[]{:S(2)}) copy-start(s32[1024]{0:T(1024)} %param.23) | copy-start | bytes 12292
  7.2 10.9 %copy-start.4 = (s32[1024]{0:T(1024)S(1)}, s32[1024]{0:T(1024)}, u32[]{:S(2)}) copy-start(s32[1024]{0:T(1024)} %param.24) | copy-start | bytes 12292
  7.2 57.8 %all-gather.3.cloned.1.call-start = ((), (), s32[]{:S(2)}) async-start(), calls=%async_computation.4 | async-start | bytes 1572864 | tf_op jit(solution)/shard_map/all_gather | solution.py:102
  8.7 9.6 %copy-start.6 = (f32[2,256]{1,0:T(2,128)S(1)}, f32[2,256]{1,0:T(2,128)}, u32[]{:S(2)}) copy-start(f32[2,256]{1,0:T(2,128)} %param.27) | copy-start | bytes 6148
  11.0 49.7 %collective-permute-start = (bf16[256,128]{0,1:T(8,128)(2,1)S(1)}, bf16[256,128]{0,1:T(8,128)(2,1)S(1)}, u32[]{:S(2)}, u32[]{:S(2)}) collective-permute-start(bf16[256,128]{0,1:T(8,128)(2,1)S(1)} %convolution_convert_fusion.9), channel_id=1, source_target_pairs={{0,2},{2,4},{4,6},{6,8},{8,10},{10,12},{12,14},{14,16},{16,18},{18... | collective-permute-start | bytes 196616 | tf_op jit(solution)/shard_map/ppermute | solution.py:16
  13.9 46.9 %collective-permute-start.1 = (bf16[256,128]{0,1:T(8,128)(2,1)S(1)}, bf16[256,128]{0,1:T(8,128)(2,1)S(1)}, u32[]{:S(2)}, u32[]{:S(2)}) collective-permute-start(bf16[256,128]{0,1:T(8,128)(2,1)S(1)} %convolution_convert_fusion.9), channel_id=1, source_target_pairs={{2,0},{4,2},{6,4},{8,6},{10,8},{12,10},{14,12},{16,14},{18,16},{20... | collective-permute-start | bytes 196616 | tf_op jit(solution)/shard_map/ppermute | solution.py:17
  18.0 54.8 %reduce-scatter.5.cloned.1.call-start = ((), (), s32[]{:S(2)}) async-start(), calls=%async_computation.5 | async-start | bytes 1572864 | tf_op jit(solution)/shard_map/reduce_scatter | solution.py:114
  65.0 3.4 %copy-start.2 = (bf16[256,1024]{1,0:T(8,128)(2,1)S(1)}, bf16[256,1024]{1,0:T(8,128)(2,1)}, u32[]{:S(2)}) copy-start(bf16[256,1024]{1,0:T(8,128)(2,1)} %param.22) | copy-start | bytes 1572868
  68.3 1.0 copy-start.8
  68.3 1.0 copy-start.9
  68.3 1.0 copy-start.10
  68.3 1.1 copy-start.11
  68.3 23.4 %reduce-scatter.7.cloned.1.call-start = ((), (), s32[]{:S(2)}) async-start(), calls=%async_computation.6 | async-start | bytes 196608 | tf_op jit(solution)/shard_map/reduce_scatter | solution.py:140
  78.5 4.6 %copy-start = (bf16[256,1024]{0,1:T(8,128)(2,1)}, bf16[256,1024]{0,1:T(8,128)(2,1)S(1)}, u32[]{:S(2)}) copy-start(bf16[256,1024]{0,1:T(8,128)(2,1)S(1)} %select_convert_fusion.1) | copy-start | bytes 1572868
  78.5 4.4 %copy-start.12 = (f32[2,256]{1,0:T(2,128)S(1)}, f32[2,256]{1,0:T(2,128)}, u32[]{:S(2)}) copy-start(f32[2,256]{1,0:T(2,128)} %param.36) | copy-start | bytes 6148
  78.5 4.5 %copy-start.13 = (f32[2,256]{1,0:T(2,128)S(1)}, f32[2,256]{1,0:T(2,128)}, u32[]{:S(2)}) copy-start(f32[2,256]{1,0:T(2,128)} %param.37) | copy-start | bytes 6148
  82.8 67.6 %all-gather.5.cloned.1.call-start = ((), (), s32[]{:S(2)}) async-start(), calls=%async_computation.7 | async-start | bytes 1572864 | tf_op jit(solution)/shard_map/all_gather | solution.py:102
  83.4 75.0 %reduce-scatter.9.cloned.1.call-start = ((), (), s32[]{:S(2)}) async-start(), calls=%async_computation.8 | async-start | bytes 1572864 | tf_op jit(solution)/shard_map/reduce_scatter | solution.py:114
  98.3 48.0 %collective-permute-start.2 = (bf16[256,128]{0,1:T(8,128)(2,1)S(1)}, bf16[256,128]{0,1:T(8,128)(2,1)S(1)}, u32[]{:S(2)}, u32[]{:S(2)}) collective-permute-start(bf16[256,128]{0,1:T(8,128)(2,1)S(1)} %fusion.13), channel_id=1, source_target_pairs={{0,2},{2,4},{4,6},{6,8},{8,10},{10,12},{12,14},{14,16},{16,18},{18... | collective-permute-start | bytes 196616 | tf_op jit(solution)/shard_map/ppermute | solution.py:16
  100.0 46.3 %collective-permute-start.3 = (bf16[256,128]{0,1:T(8,128)(2,1)S(1)}, bf16[256,128]{0,1:T(8,128)(2,1)S(1)}, u32[]{:S(2)}, u32[]{:S(2)}) collective-permute-start(bf16[256,128]{0,1:T(8,128)(2,1)S(1)} %fusion.13), channel_id=1, source_target_pairs={{2,0},{4,2},{6,4},{8,6},{10,8},{12,10},{14,12},{16,14},{18,16},{20... | collective-permute-start | bytes 196616 | tf_op jit(solution)/shard_map/ppermute | solution.py:17
  153.8 8.6 %copy-start.1 = (bf16[256,1024]{0,1:T(8,128)(2,1)S(1)}, bf16[256,1024]{0,1:T(8,128)(2,1)}, u32[]{:S(2)}) copy-start(bf16[256,1024]{0,1:T(8,128)(2,1)} %copy-done) | copy-start | bytes 1572868
  153.8 22.7 %reduce-scatter.11.cloned.1.call-start = ((), (), s32[]{:S(2)}) async-start(), calls=%async_computation.9 | async-start | bytes 196608 | tf_op jit(solution)/shard_map/reduce_scatter | solution.py:140
  158.4 8.1 %copy-start.14 = (bf16[2,256,512]{2,1,0:T(8,128)(2,1)S(1)}, bf16[2,256,512]{2,1,0:T(8,128)(2,1)}, u32[]{:S(2)}) copy-start(bf16[2,256,512]{2,1,0:T(8,128)(2,1)} %param.34) | copy-start | bytes 1572868
  (1 other events, 1.0 us)
Sparse Core Ops, SparseCore 0:
  18.1 6.7 all-gather.2
  68.5 4.2 reduce-scatter.4
  83.0 8.7 reduce-scatter.6
  93.7 9.8 all-gather.4
  154.0 4.4 reduce-scatter.8
  167.8 8.7 reduce-scatter.10
where the time goes:
time: 189 us
  blocking collectives  93.7 us (50%)
  waiting for transfers between devices  22.6 us (12%)
  local copies, waits for them, and re-layouts  21.9 us (12%)
  between operations  15.3 us (8%)
  starting transfers between devices  12.9 us (7%)
  matrix products  11.7 us (6%)
  other arithmetic  10.5 us (6%)
    all_gather x2, blocking collectives, on_device(): lax.all_gather(sender_part[:, :coarse_rows], 'patch', axis=1, tiled=True)  76 us
    reduce_scatter x2, waiting for transfers between devices, on_device(): lax.psum_scatter(node_partial.astype(jnp.bfloat16), 'width', scatter_dime...  16.2 us
    dot_general x4, matrix products, contract_first(): lax.dot_general(left, right, (((0,), (0,)), ((), ())), preferred_element_...  9.74 us
    gather x4, local copies, waits for them, and re-layouts, on_device(): jnp.take(receiver_part, local_receiver, axis=1).astype(jnp.float32)  8.3 us
    gather x4, local copies, waits for them, and re-layouts, on_device(): jnp.take(table, sender_index, axis=1).astype(jnp.float32)  8.3 us
    ppermute x2, starting transfers between devices, with_halo(): after = lax.ppermute(initial, axis, down)  8 us
    reduce_scatter x2, waiting for transfers between devices, on_device(): lax.psum_scatter(edge_partial.astype(jnp.bfloat16), 'width', scatter_dime...  5.92 us
    psum x2, blocking collectives, on_device(): lax.psum((jnp.sum(edge_mlp, axis=0), jnp.sum(edge_mlp * edge_mlp, axis=0)...  4.99 us
  transfers between devices with their start and end apart: 10, of which 4 were waited for; matrix products, arithmetic and copies ran while one was open for 12% of the time, Pallas kernels for 0%

commit v1 on v0

v1 whole, which is shorter than its diff:
```python
import functools

import jax
import jax.numpy as jnp
from jax import lax
from jax.experimental import pallas as pl
from jax.experimental.pallas import tpu as pltpu
from jax.sharding import PartitionSpec as P

MESH = pl.DeviceIdType.MESH
epsilon = 1e-05
bf16 = jnp.bfloat16
f32 = jnp.float32


def dot(left, right, dims=((1,), (0,))):
    return lax.dot_general(left, right, (dims, ((), ())), preferred_element_type=f32)


def silu(v):
    h = 0.5 * v
    return h + h * jnp.tanh(h)


def layer_norm(values, gain, shift):
    width = values.shape[0]
    mean = jnp.sum(values, axis=0, keepdims=True) / width
    square = jnp.sum(values * values, axis=0, keepdims=True) / width
    return (values - mean) * lax.rsqrt(square - mean * mean + epsilon) * gain + shift


def kernel(
    patches,
    nodes_in,
    edges_in,
    senders_ref,
    receivers_ref,
    count_ref,
    wi_in,
    wo_in,
    vi_in,
    vo_in,
    *rest,
):
    vector_in = rest[:8]
    nodes_out, edges_out = rest[8:10]
    (
        nodes,
        edges,
        wi,
        wo,
        vi,
        vo,
        vectors,
        columns,
        halo,
        coarse,
        part_send,
        coarse_send,
        agg_send,
        agg_recv,
        own,
        hot_own,
        hot_halo,
        hot_coarse,
        incidence,
        before,
        local_sem,
        w_send,
        w_recv,
        halo_send,
        halo_recv,
        coarse_send_sem,
        coarse_recv_sem,
        relay_send,
        relay_recv,
        agg_sems,
        out_sems,
    ) = rest[10:]
    layers = wi.shape[0]
    half = nodes_in.shape[0]
    width = 2 * half
    rows = nodes_in.shape[1]
    slots = edges_in.shape[1]
    mine = slots // 2
    top = coarse_send.shape[1]
    far = patches - 3

    me = lax.axis_index("patch")
    core = lax.axis_index("width")
    other = 1 - core
    here = pl.ds(pl.multiple_of(core * half, half), half)
    there = pl.ds(pl.multiple_of(other * half, half), half)
    my_slots = pl.ds(pl.multiple_of(core * mine, mine), mine)
    other_slots = pl.ds(pl.multiple_of(other * mine, mine), mine)

    def local(src, dst, index):
        return pltpu.make_async_copy(src, dst, local_sem.at[index])

    def remote(src, dst, send, recv, patch, width_index):
        return pltpu.make_async_remote_copy(
            src_ref=src,
            dst_ref=dst,
            send_sem=send,
            recv_sem=recv,
            device_id={"patch": patch, "width": width_index},
            device_id_type=MESH,
        )

    blocks = [
        (nodes_in, nodes.at[here], nodes_in, nodes.at[there]),
        (edges_in.at[:, my_slots], edges.at[here], edges_in.at[:, other_slots], edges.at[there]),
    ]
    place = {"nodes": 0, "edges": 1}
    for layer in range(layers):
        for name, source, target in (("wi", wi_in, wi), ("wo", wo_in, wo), ("vi", vi_in, vi), ("vo", vo_in, vo)):
            place[name, layer] = len(blocks)
            blocks.append(
                (source.at[layer], target.at[layer, here], source.at[layer], target.at[layer, there])
            )
        if layer == 0:
            place["vectors"] = len(blocks)
            for index, source in enumerate(vector_in):
                blocks.append(
                    (source, vectors.at[index, :, here], source, vectors.at[index, :, there])
                )

    locals_ = [local(b[0], b[1], i) for i, b in enumerate(blocks)]
    for copy in locals_:
        copy.start()

    def greet(step, carry):
        target = lax.rem(me + step, patches)
        pl.semaphore_signal(
            pltpu.get_barrier_semaphore(), inc=1, device_id={"patch": target, "width": core}, device_id_type=MESH
        )
        return carry

    barrier = pltpu.get_barrier_semaphore()
    pl.semaphore_signal(barrier, inc=1, device_id={"patch": me, "width": other}, device_id_type=MESH)
    lax.fori_loop(1, patches, greet, 0)

    sender = senders_ref[:, my_slots]
    receiver = receivers_ref[:, my_slots] - me * rows
    slot = lax.broadcasted_iota(jnp.int32, (1, mine), 1) + core * mine
    live = slot < count_ref[0]
    owner = sender // rows
    within = sender - owner * rows
    distance = lax.rem(me - owner + patches, patches)
    node_iota = lax.broadcasted_iota(jnp.int32, (rows, mine), 0)

    def hot(index, iota):
        return jnp.where(iota == index, 1.0, 0.0).astype(bf16)

    hot_own[:rows] = hot(jnp.where(distance == 0, within, -1), node_iota)
    hot_own[rows:] = hot(receiver, node_iota)
    hot_halo[:rows] = hot(jnp.where(distance == 1, within, -1), node_iota)
    hot_halo[rows:] = hot(jnp.where(distance == patches - 1, within, -1), node_iota)
    far_index = jnp.where((distance >= 2) & (distance <= patches - 2), (distance - 2) * top + within, -1)
    hot_coarse[...] = hot(far_index, lax.broadcasted_iota(jnp.int32, hot_coarse.shape, 0))
    incidence[...] = hot(jnp.where(live, receiver, -1), node_iota)
    pad = coarse.shape[2] - far * top
    if pad:
        for layer in range(layers):
            for part in range(2):
                coarse[layer, part, far * top :, :] = jnp.zeros((pad, half), bf16)

    pl.semaphore_wait(barrier, patches)

    remotes = []
    for i, b in enumerate(blocks):
        target = b[1]
        remotes.append(remote(b[2], target, w_send.at[i], w_recv.at[i], me, other))
    for copy in remotes:
        copy.start()

    def arrive(index):
        locals_[index].wait()
        b = blocks[index]
        remote(b[3], b[3], w_send.at[index], w_recv.at[index], me, other).wait_recv()

    def column(index, layer):
        position = index * layers + layer
        return columns[:, position : position + 1]

    waited_out = []
    for layer in range(layers):
        if layer == 0:
            arrive(place["nodes"])
        locals_[place["wi", layer]].wait()
        part = dot(wi[layer, here, width : 2 * width], nodes[...])
        part_send[layer] = part.astype(bf16)
        up = remote(
            part_send.at[layer],
            halo.at[layer, here, pl.ds(0, rows)],
            halo_send.at[layer, 0],
            halo_recv.at[layer, 0],
            lax.rem(me + 1, patches),
            core,
        )
        down = remote(
            part_send.at[layer],
            halo.at[layer, here, pl.ds(rows, rows)],
            halo_send.at[layer, 1],
            halo_recv.at[layer, 1],
            lax.rem(me + patches - 1, patches),
            core,
        )
        up.start()
        down.start()
        coarse_send[layer] = part.T[:top].astype(bf16)

        def spread(step, carry):
            remote(
                coarse_send.at[layer],
                coarse.at[layer, core, pl.ds(pl.multiple_of((step - 2) * top, top), top)],
                coarse_send_sem.at[layer],
                coarse_recv_sem.at[layer],
                lax.rem(me + step, patches),
                core,
            ).start()
            return carry

        lax.fori_loop(2, patches - 1, spread, 0)

        b = blocks[place["wi", layer]]
        index = place["wi", layer]
        remote(b[3], b[3], w_send.at[index], w_recv.at[index], me, other).wait_recv()
        own[:, :rows] = dot(wi[layer, :, width : 2 * width], nodes[...]).astype(bf16)
        own[:, rows:] = dot(wi[layer, :, 2 * width :], nodes[...]).astype(bf16)
        if layer == 0:
            arrive(place["edges"])
            for k in range(8):
                arrive(place["vectors"] + k)
            flat = vectors[...].reshape(8 * layers, width)
            columns[...] = flat.T
        before[...] = (
            dot(wi[layer, :, :width], edges[...]) + dot(own[...], hot_own[...]) + column(0, layer)
        )
        arrive(place["vi", layer])
        node_first = dot(vi[layer, :, :width], nodes[...]) + column(4, layer)

        up.wait_recv()
        down.wait_recv()
        relay_halo = remote(
            halo.at[layer, here], halo.at[layer, here], relay_send.at[layer, 0], relay_recv.at[layer, 0], me, other
        )
        relay_halo.start()
        every = coarse.at[layer, core, pl.ds(0, far * top)]
        all_coarse = remote(every, every, coarse_send_sem.at[layer], coarse_recv_sem.at[layer], me, other)
        all_coarse.wait_recv()
        relay_coarse = remote(
            every, every, relay_send.at[layer, 1], relay_recv.at[layer, 1], me, other
        )
        relay_coarse.start()
        before[here, :] = (
            before[here, :]
            + dot(halo[layer, here, :], hot_halo[...])
            + dot(coarse[layer, core], hot_coarse[...], ((0,), (0,)))
        )
        arrive(place["wo", layer])
        from_halo = halo.at[layer, there]
        remote(from_halo, from_halo, relay_send.at[layer, 0], relay_recv.at[layer, 0], me, other).wait_recv()
        from_coarse = coarse.at[layer, other, pl.ds(0, far * top)]
        remote(from_coarse, from_coarse, relay_send.at[layer, 1], relay_recv.at[layer, 1], me, other).wait_recv()
        before[there, :] = (
            before[there, :]
            + dot(halo[layer, there, :], hot_halo[...])
            + dot(coarse[layer, other], hot_coarse[...], ((0,), (0,)))
        )

        hidden = silu(before[...]).astype(bf16)
        mlp = dot(wo[layer], hidden, ((0,), (0,))) + column(1, layer)
        updated = edges[...].astype(f32) + layer_norm(mlp, column(2, layer), column(3, layer))
        edges[...] = jnp.where(live, updated, 0.0).astype(bf16)
        partial = dot(edges[...], incidence[...], ((1,), (1,)))
        agg_send[layer] = partial.astype(bf16)
        swap = remote(
            agg_send.at[layer], agg_recv.at[layer], agg_sems.at[layer, 0], agg_sems.at[layer, 1], me, other
        )
        swap.start()
        if layer == layers - 1:
            keep = pltpu.make_async_copy(edges.at[here], edges_out.at[:, my_slots], out_sems.at[0])
            keep.start()
            give = remote(
                edges.at[there], edges_out.at[:, my_slots], out_sems.at[1], out_sems.at[2], me, other
            )
            give.start()
        arrive(place["vo", layer])
        swap.wait_recv()
        aggregate = (partial + agg_recv[layer].astype(f32)).astype(bf16)
        node_hidden = silu(node_first + dot(vi[layer, :, width:], aggregate)).astype(bf16)
        node_mlp = dot(vo[layer], node_hidden, ((0,), (0,))) + column(5, layer)
        nodes[...] = (
            nodes[...].astype(f32) + layer_norm(node_mlp, column(6, layer), column(7, layer))
        ).astype(bf16)
        waited_out += [up, down, all_coarse, relay_halo, relay_coarse, swap]

    store = pltpu.make_async_copy(nodes.at[here], nodes_out, out_sems.at[3])
    store.start()
    for copy in remotes + waited_out:
        copy.wait_send()
    keep.wait()
    give.wait_send()
    got = edges_out.at[:, other_slots]
    remote(got, got, out_sems.at[1], out_sems.at[2], me, other).wait_recv()
    store.wait()


def on_device(
    patches,
    node_latents,
    edge_latents,
    senders,
    receivers,
    edge_count,
    edge_in_weight,
    edge_in_bias,
    edge_out_weight,
    edge_out_bias,
    edge_gain,
    edge_shift,
    node_in_weight,
    node_in_bias,
    node_out_weight,
    node_out_bias,
    node_gain,
    node_shift,
):
    half, rows = node_latents.shape
    slots = edge_latents.shape[1]
    layers = edge_in_weight.shape[0]
    width = 2 * half
    mine = slots // 2
    top = rows // 8
    far_rows = -(-(patches - 3) * top // 128) * 128
    vmem = pltpu.VMEM
    dma = pltpu.SemaphoreType.DMA
    copies = 2 + 4 * layers + 8
    anywhere = pl.BlockSpec(memory_space=pl.ANY)
    return pl.pallas_call(
        functools.partial(kernel, patches),
        out_shape=(
            jax.ShapeDtypeStruct((half, rows), bf16),
            jax.ShapeDtypeStruct((half, slots), bf16),
        ),
        in_specs=[anywhere, anywhere]
        + [pl.BlockSpec(memory_space=vmem)] * 2
        + [pl.BlockSpec(memory_space=pltpu.SMEM)]
        + [anywhere] * 12,
        out_specs=(anywhere, anywhere),
        scratch_shapes=[
            vmem((width, rows), bf16),
            vmem((width, mine), bf16),
            vmem((layers, width, 3 * width), bf16),
            vmem((layers, width, width), bf16),
            vmem((layers, width, 2 * width), bf16),
            vmem((layers, width, width), bf16),
            vmem((8, layers, width), f32),
            vmem((width, 8 * layers), f32),
            vmem((layers, width, 2 * rows), bf16),
            vmem((layers, 2, far_rows, half), bf16),
            vmem((layers, half, rows), bf16),
            vmem((layers, top, half), bf16),
            vmem((layers, width, rows), bf16),
            vmem((layers, width, rows), bf16),
            vmem((width, 2 * rows), bf16),
            vmem((2 * rows, mine), bf16),
            vmem((2 * rows, mine), bf16),
            vmem((far_rows, mine), bf16),
            vmem((rows, mine), bf16),
            vmem((width, mine), f32),
            dma((copies,)),
            dma((copies,)),
            dma((copies,)),
            dma((layers, 2)),
            dma((layers, 2)),
            dma((layers,)),
            dma((layers,)),
            dma((layers, 2)),
            dma((layers, 2)),
            dma((layers, 2)),
            dma((4,)),
        ],
        compiler_params=pltpu.CompilerParams(collective_id=0, has_side_effects=True, vmem_limit_bytes=56 * 2**20),
    )(
        node_latents,
        edge_latents,
        senders.reshape(1, slots),
        receivers.reshape(1, slots),
        edge_count,
        edge_in_weight,
        edge_out_weight,
        node_in_weight,
        node_out_weight,
        edge_in_bias,
        edge_out_bias,
        edge_gain,
        edge_shift,
        node_in_bias,
        node_out_bias,
        node_gain,
        node_shift,
    )


def solution(mesh):
    by_width = P(None, "width")
    return jax.shard_map(
        functools.partial(on_device, mesh.shape["patch"]),
        mesh=mesh,
        in_specs=(
            P("width", "patch"),
            P("width", "patch"),
            P("patch"),
            P("patch"),
            P("patch"),
            P(None, "width", None),
            by_width,
            P(None, "width", None),
            by_width,
            by_width,
            by_width,
            P(None, "width", None),
            by_width,
            P(None, "width", None),
            by_width,
            by_width,
            by_width,
        ),
        out_specs=(P("width", "patch"), P("width", "patch")),
        check_vma=False,
    )
```

time: 189 us -> 37.2 us (0.20)
  blocking collectives: 93.7 us -> 0 us
  Pallas kernels: 0 us -> 32.3 us
  waiting for transfers between devices: 22.6 us -> 0 us
  local copies, waits for them, and re-layouts: 21.9 us -> 3.34 us
  between operations: 15.3 us -> 1.29 us
  starting transfers between devices: 12.9 us -> 0 us
  matrix products: 11.7 us -> 0 us
  other arithmetic: 10.5 us -> 0 us
    all_gather x6 -> x0, blocking collectives: 83.8 us -> none  [the longest x2 76 us: on_device(): lax.all_gather(sender_part[:, :coarse_rows], 'patch', axis=1, tiled=True)]
    pallas_call x0 -> x1, Pallas kernels: none -> 32.3 us  [on_device(): pl.pallas_call(functools.partial(kernel, patches), out_shape=(jax.ShapeDt...]
    reduce_scatter x4 -> x0, waiting for transfers between devices: 22.1 us -> none  [the longest x2 16.2 us: on_device(): lax.psum_scatter(node_partial.astype(jnp.bfloat16), 'width', scatter_dime...]
    gather x8 -> x0, local copies, waits for them, and re-layouts: 16.6 us -> none  [the longest x4 8.3 us: on_device(): jnp.take(receiver_part, local_receiver, axis=1).astype(jnp.float32)]
    ppermute x4 -> x0, starting transfers between devices: 12.6 us -> none  [the longest x2 8 us: with_halo(): after = lax.ppermute(initial, axis, down)]
    dot_general x12 -> x0, matrix products: 11.7 us -> none  [the longest x4 9.74 us: contract_first(): lax.dot_general(left, right, (((0,), (0,)), ((), ())), preferred_element_...]
    psum x4 -> x0, blocking collectives: 9.94 us -> none  [the longest x2 4.99 us: on_device(): lax.psum((jnp.sum(edge_mlp, axis=0), jnp.sum(edge_mlp * edge_mlp, axis=0)...]
    convert_element_type x4 -> x0, other arithmetic: 5.6 us -> none  [the longest x2 3.7 us: on_device(): jnp.where(live[None, :], updated, jnp.float32(0.0)).astype(jnp.bfloat16)]
  transfers between devices with their start and end apart: 10 -> 0, of which waited for: 4 -> 0; matrix products, arithmetic and copies ran while one was open for 12% -> 0% of each run, Pallas kernels for 0% -> 0%
where the time goes in v1:
time: 37.2 us; the launch traced here: 37 us
  Pallas kernels  32.3 us (87%)
  local copies, waits for them, and re-layouts  3.34 us (9%)
  between operations  1.29 us (3%)
    pallas_call x1, Pallas kernels, on_device(): pl.pallas_call(functools.partial(kernel, patches), out_shape=(jax.ShapeDt...  32.3 us
    unnamed x2, local copies, waits for them, and re-layouts  3.34 us

profile of v1, /device:TPU:0, one launch (start us, length us, event | category | flops | bytes accessed | tf_op | source)
XLA Modules:
  0.0 37.0 jit_solution(10177289857334198916)
XLA Ops:
  1.3 32.3 %shard_map.176 = (bf16[256,128]{1,0:T(8,128)(2,1)}, bf16[256,1024]{1,0:T(8,128)(2,1)}) custom-call(bf16[256,128]{1,0:T(8,128)(2,1)} %nodes_in.1, bf16[256,1024]{1,0:T(8,128)(2,1)} %edges_in.1, s32[1,1024]{1,0:T(1,128)} %bitcast.2, s32[1,1024]{1,0:T(1,128)} %bitcast.3, s32[1]{0:T(128)S(6)} %copy.21.count_ref, bf16[2,256,1536]{2,1,0:T(8,128)(2,1)} %wi_in.1, ...), custom_call_target="tpu_custom_call" | custom-call | tf_op jit(solution)/shard_map/pallas_call | solution.py:341
  33.6 1.5 %copy.22 = bf16[256,128]{1,0:T(8,128)(2,1)} copy(bf16[256,128]{1,0:T(8,128)(2,1)} %get-tuple-element.4) | data formatting | bytes 131072
  35.1 1.9 %copy.23 = bf16[256,1024]{1,0:T(8,128)(2,1)} copy(bf16[256,1024]{1,0:T(8,128)(2,1)} %get-tuple-element.5) | data formatting | bytes 1048576

commit v2 on v1

--- a/solution.py
+++ b/solution.py
@@ -33,9 +33,9 @@
     patches,
     nodes_in,
     edges_in,
-    senders_ref,
-    receivers_ref,
-    count_ref,
+    senders_in,
+    receivers_in,
+    count_in,
     wi_in,
     wo_in,
     vi_in,
@@ -60,11 +60,17 @@
         agg_send,
         agg_recv,
         own,
+        table,
         hot_own,
-        hot_halo,
-        hot_coarse,
+        hot_far,
         incidence,
         before,
+        senders_ref,
+        receivers_ref,
+        count_ref,
+        wo_turned,
+        vo_turned,
+        graph_sem,
         local_sem,
         w_send,
         w_recv,
@@ -125,10 +131,6 @@
                     (source, vectors.at[index, :, here], source, vectors.at[index, :, there])
                 )
 
-    locals_ = [local(b[0], b[1], i) for i, b in enumerate(blocks)]
-    for copy in locals_:
-        copy.start()
-
     def greet(step, carry):
         target = lax.rem(me + step, patches)
         pl.semaphore_signal(
@@ -139,6 +141,21 @@
     barrier = pltpu.get_barrier_semaphore()
     pl.semaphore_signal(barrier, inc=1, device_id={"patch": me, "width": other}, device_id_type=MESH)
     lax.fori_loop(1, patches, greet, 0)
+
+    graph = [
+        pltpu.make_async_copy(source, target, graph_sem.at[i])
+        for i, (source, target) in enumerate(
+            ((senders_in, senders_ref), (receivers_in, receivers_ref), (count_in, count_ref))
+        )
+    ]
+    locals_ = [local(b[0], b[1], i) for i, b in enumerate(blocks)]
+    locals_[0].start()
+    for copy in graph + locals_[1:]:
+        copy.start()
+    locals_[0].wait()
+    coarse_send[0] = nodes[here, :].astype(f32).T[:top].astype(bf16)
+    for copy in graph:
+        copy.wait()
 
     sender = senders_ref[:, my_slots]
     receiver = receivers_ref[:, my_slots] - me * rows
@@ -154,10 +171,10 @@
 
     hot_own[:rows] = hot(jnp.where(distance == 0, within, -1), node_iota)
     hot_own[rows:] = hot(receiver, node_iota)
-    hot_halo[:rows] = hot(jnp.where(distance == 1, within, -1), node_iota)
-    hot_halo[rows:] = hot(jnp.where(distance == patches - 1, within, -1), node_iota)
+    hot_far[:rows] = hot(jnp.where(distance == 1, within, -1), node_iota)
+    hot_far[rows : 2 * rows] = hot(jnp.where(distance == patches - 1, within, -1), node_iota)
     far_index = jnp.where((distance >= 2) & (distance <= patches - 2), (distance - 2) * top + within, -1)
-    hot_coarse[...] = hot(far_index, lax.broadcasted_iota(jnp.int32, hot_coarse.shape, 0))
+    hot_far[2 * rows :] = hot(far_index, lax.broadcasted_iota(jnp.int32, (coarse.shape[2], mine), 0))
     incidence[...] = hot(jnp.where(live, receiver, -1), node_iota)
     pad = coarse.shape[2] - far * top
     if pad:
@@ -167,49 +184,23 @@
 
     pl.semaphore_wait(barrier, patches)
 
-    remotes = []
-    for i, b in enumerate(blocks):
-        target = b[1]
-        remotes.append(remote(b[2], target, w_send.at[i], w_recv.at[i], me, other))
-    for copy in remotes:
-        copy.start()
-
-    def arrive(index):
-        locals_[index].wait()
-        b = blocks[index]
-        remote(b[3], b[3], w_send.at[index], w_recv.at[index], me, other).wait_recv()
-
-    def column(index, layer):
-        position = index * layers + layer
-        return columns[:, position : position + 1]
-
-    waited_out = []
-    for layer in range(layers):
-        if layer == 0:
-            arrive(place["nodes"])
-        locals_[place["wi", layer]].wait()
-        part = dot(wi[layer, here, width : 2 * width], nodes[...])
-        part_send[layer] = part.astype(bf16)
-        up = remote(
-            part_send.at[layer],
-            halo.at[layer, here, pl.ds(0, rows)],
-            halo_send.at[layer, 0],
-            halo_recv.at[layer, 0],
-            lax.rem(me + 1, patches),
-            core,
-        )
-        down = remote(
-            part_send.at[layer],
-            halo.at[layer, here, pl.ds(rows, rows)],
-            halo_send.at[layer, 1],
-            halo_recv.at[layer, 1],
-            lax.rem(me + patches - 1, patches),
-            core,
-        )
-        up.start()
-        down.start()
-        coarse_send[layer] = part.T[:top].astype(bf16)
-
+    def send_far(layer, source):
+        copies = [
+            remote(
+                source,
+                halo.at[layer, here, pl.ds(side * rows, rows)],
+                halo_send.at[layer, side],
+                halo_recv.at[layer, side],
+                lax.rem(me + step, patches),
+                core,
+            )
+            for side, step in enumerate((1, patches - 1))
+        ]
+        for copy in copies:
+            copy.start()
+        return copies
+
+    def spread_coarse(layer):
         def spread(step, carry):
             remote(
                 coarse_send.at[layer],
@@ -223,10 +214,40 @@
 
         lax.fori_loop(2, patches - 1, spread, 0)
 
-        b = blocks[place["wi", layer]]
-        index = place["wi", layer]
+    sent_far = send_far(0, nodes.at[here])
+    spread_coarse(0)
+    remotes = [
+        remote(b[2], b[1], w_send.at[i], w_recv.at[i], me, other) for i, b in enumerate(blocks)
+    ]
+    for copy in remotes:
+        copy.start()
+
+    def arrive(index):
+        if index:
+            locals_[index].wait()
+        b = blocks[index]
         remote(b[3], b[3], w_send.at[index], w_recv.at[index], me, other).wait_recv()
-        own[:, :rows] = dot(wi[layer, :, width : 2 * width], nodes[...]).astype(bf16)
+
+    def column(index, layer):
+        position = index * layers + layer
+        return columns[:, position : position + 1]
+
+    waited_out = []
+    sender_columns = slice(width, 2 * width)
+    wide = [(k * mine // 2, (k + 1) * mine // 2) for k in range(2)]
+    for layer in range(layers):
+        if layer:
+            arrive(place["wi", layer])
+            part = dot(wi[layer, here, sender_columns], nodes[...])
+            part_send[layer] = part.astype(bf16)
+            sent_far = send_far(layer, part_send.at[layer])
+            coarse_send[layer] = part.T[:top].astype(bf16)
+            spread_coarse(layer)
+        else:
+            arrive(place["nodes"])
+            arrive(place["wi", layer])
+
+        own[:, :rows] = dot(wi[layer, :, sender_columns], nodes[...]).astype(bf16)
         own[:, rows:] = dot(wi[layer, :, 2 * width :], nodes[...]).astype(bf16)
         if layer == 0:
             arrive(place["edges"])
@@ -239,41 +260,68 @@
         )
         arrive(place["vi", layer])
         node_first = dot(vi[layer, :, :width], nodes[...]) + column(4, layer)
-
-        up.wait_recv()
-        down.wait_recv()
-        relay_halo = remote(
-            halo.at[layer, here], halo.at[layer, here], relay_send.at[layer, 0], relay_recv.at[layer, 0], me, other
-        )
-        relay_halo.start()
+        arrive(place["wo", layer])
+        wo_turned[...] = wo[layer].T
+        arrive(place["vo", layer])
+        vo_turned[...] = vo[layer].T
+
+        relays = []
+
+        def passed(index, ref):
+            return remote(ref, ref, relay_send.at[layer, index], relay_recv.at[layer, index], me, other)
+
+        for side in range(2):
+            sent_far[side].wait_recv()
+            relays.append(passed(side, halo.at[layer, here, pl.ds(side * rows, rows)]))
+            relays[-1].start()
         every = coarse.at[layer, core, pl.ds(0, far * top)]
         all_coarse = remote(every, every, coarse_send_sem.at[layer], coarse_recv_sem.at[layer], me, other)
         all_coarse.wait_recv()
-        relay_coarse = remote(
-            every, every, relay_send.at[layer, 1], relay_recv.at[layer, 1], me, other
-        )
-        relay_coarse.start()
-        before[here, :] = (
-            before[here, :]
-            + dot(halo[layer, here, :], hot_halo[...])
-            + dot(coarse[layer, core], hot_coarse[...], ((0,), (0,)))
-        )
-        arrive(place["wo", layer])
-        from_halo = halo.at[layer, there]
-        remote(from_halo, from_halo, relay_send.at[layer, 0], relay_recv.at[layer, 0], me, other).wait_recv()
-        from_coarse = coarse.at[layer, other, pl.ds(0, far * top)]
-        remote(from_coarse, from_coarse, relay_send.at[layer, 1], relay_recv.at[layer, 1], me, other).wait_recv()
-        before[there, :] = (
-            before[there, :]
-            + dot(halo[layer, there, :], hot_halo[...])
-            + dot(coarse[layer, other], hot_coarse[...], ((0,), (0,)))
-        )
-
-        hidden = silu(before[...]).astype(bf16)
-        mlp = dot(wo[layer], hidden, ((0,), (0,))) + column(1, layer)
-        updated = edges[...].astype(f32) + layer_norm(mlp, column(2, layer), column(3, layer))
-        edges[...] = jnp.where(live, updated, 0.0).astype(bf16)
-        partial = dot(edges[...], incidence[...], ((1,), (1,)))
+        relays.append(passed(2, every))
+        relays[-1].start()
+
+        if layer == 0:
+            senders_here = wi[layer, :, pl.ds(pl.multiple_of(width + core * half, half), half)]
+            senders_there = wi[layer, :, pl.ds(pl.multiple_of(width + other * half, half), half)]
+            table[:, : 2 * rows] = dot(senders_here, halo[layer, here, :])
+            table[:, 2 * rows :] = dot(senders_here, coarse[layer, core], ((1,), (1,)))
+        else:
+            before[here, :] = (
+                before[here, :]
+                + dot(halo[layer, here, :], hot_far[: 2 * rows])
+                + dot(coarse[layer, core], hot_far[2 * rows :], ((0,), (0,)))
+            )
+        for side in range(2):
+            passed(side, halo.at[layer, there, pl.ds(side * rows, rows)]).wait_recv()
+        passed(2, coarse.at[layer, other, pl.ds(0, far * top)]).wait_recv()
+        if layer == 0:
+            near = (table[:, : 2 * rows] + dot(senders_there, halo[layer, there, :])).astype(bf16)
+            away = (
+                table[:, 2 * rows :] + dot(senders_there, coarse[layer, other], ((1,), (1,)))
+            ).astype(bf16)
+        else:
+            before[there, :] = (
+                before[there, :]
+                + dot(halo[layer, there, :], hot_far[: 2 * rows])
+                + dot(coarse[layer, other], hot_far[2 * rows :], ((0,), (0,)))
+            )
+
+        partial = None
+        for low, high in wide:
+            value = before[:, low:high]
+            if layer == 0:
+                value = (
+                    value
+                    + dot(near, hot_far[: 2 * rows, low:high])
+                    + dot(away, hot_far[2 * rows :, low:high])
+                )
+            hidden = silu(value).astype(bf16)
+            mlp = dot(wo_turned[...], hidden) + column(1, layer)
+            updated = edges[:, low:high].astype(f32) + layer_norm(mlp, column(2, layer), column(3, layer))
+            fresh = jnp.where(live[:, low:high], updated, 0.0).astype(bf16)
+            edges[:, low:high] = fresh
+            term = dot(fresh, incidence[:, low:high], ((1,), (1,)))
+            partial = term if partial is None else partial + term
         agg_send[layer] = partial.astype(bf16)
         swap = remote(
             agg_send.at[layer], agg_recv.at[layer], agg_sems.at[layer, 0], agg_sems.at[layer, 1], me, other
@@ -286,15 +334,16 @@
                 edges.at[there], edges_out.at[:, my_slots], out_sems.at[1], out_sems.at[2], me, other
             )
             give.start()
-        arrive(place["vo", layer])
         swap.wait_recv()
         aggregate = (partial + agg_recv[layer].astype(f32)).astype(bf16)
         node_hidden = silu(node_first + dot(vi[layer, :, width:], aggregate)).astype(bf16)
-        node_mlp = dot(vo[layer], node_hidden, ((0,), (0,))) + column(5, layer)
+        node_mlp = dot(vo_turned[...], node_hidden) + column(5, layer)
+        for copy in sent_far:
+            copy.wait_send()
         nodes[...] = (
             nodes[...].astype(f32) + layer_norm(node_mlp, column(6, layer), column(7, layer))
         ).astype(bf16)
-        waited_out += [up, down, all_coarse, relay_halo, relay_coarse, swap]
+        waited_out += [all_coarse] + relays + [swap]
 
     store = pltpu.make_async_copy(nodes.at[here], nodes_out, out_sems.at[3])
     store.start()
@@ -305,6 +354,17 @@
     got = edges_out.at[:, other_slots]
     remote(got, got, out_sems.at[1], out_sems.at[2], me, other).wait_recv()
     store.wait()
+
+
+def put(nodes, edges, nodes_out, edges_out, sems):
+    copies = [
+        pltpu.make_async_copy(edges, edges_out, sems.at[0]),
+        pltpu.make_async_copy(nodes, nodes_out, sems.at[1]),
+    ]
+    for copy in copies:
+        copy.start()
+    for copy in copies:
+        copy.wait()
 
 
 def on_device(
@@ -338,17 +398,14 @@
     dma = pltpu.SemaphoreType.DMA
     copies = 2 + 4 * layers + 8
     anywhere = pl.BlockSpec(memory_space=pl.ANY)
-    return pl.pallas_call(
+    results = pl.pallas_call(
         functools.partial(kernel, patches),
         out_shape=(
-            jax.ShapeDtypeStruct((half, rows), bf16),
-            jax.ShapeDtypeStruct((half, slots), bf16),
+            vmem((half, rows), bf16),
+            vmem((half, slots), bf16),
         ),
-        in_specs=[anywhere, anywhere]
-        + [pl.BlockSpec(memory_space=vmem)] * 2
-        + [pl.BlockSpec(memory_space=pltpu.SMEM)]
-        + [anywhere] * 12,
-        out_specs=(anywhere, anywhere),
+        in_specs=[anywhere] * 17,
+        out_specs=(pl.BlockSpec(memory_space=vmem),) * 2,
         scratch_shapes=[
             vmem((width, rows), bf16),
             vmem((width, mine), bf16),
@@ -365,11 +422,17 @@
             vmem((layers, width, rows), bf16),
             vmem((layers, width, rows), bf16),
             vmem((width, 2 * rows), bf16),
+            vmem((width, 2 * rows + far_rows), f32),
             vmem((2 * rows, mine), bf16),
-            vmem((2 * rows, mine), bf16),
-            vmem((far_rows, mine), bf16),
+            vmem((2 * rows + far_rows, mine), bf16),
             vmem((rows, mine), bf16),
             vmem((width, mine), f32),
+            vmem((1, slots), jnp.int32),
+            vmem((1, slots), jnp.int32),
+            pltpu.SMEM((1,), jnp.int32),
+            vmem((width, width), bf16),
+            vmem((width, width), bf16),
+            dma((3,)),
             dma((copies,)),
             dma((copies,)),
             dma((copies,)),
@@ -377,8 +440,8 @@
             dma((layers, 2)),
             dma((layers,)),
             dma((layers,)),
-            dma((layers, 2)),
-            dma((layers, 2)),
+            dma((layers, 3)),
+            dma((layers, 3)),
             dma((layers, 2)),
             dma((4,)),
         ],
@@ -402,6 +465,17 @@
         node_gain,
         node_shift,
     )
+    return pl.pallas_call(
+        put,
+        out_shape=(
+            jax.ShapeDtypeStruct((half, rows), bf16),
+            jax.ShapeDtypeStruct((half, slots), bf16),
+        ),
+        in_specs=[pl.BlockSpec(memory_space=vmem)] * 2,
+        out_specs=(anywhere, anywhere),
+        scratch_shapes=[dma((2,))],
+        compiler_params=pltpu.CompilerParams(vmem_limit_bytes=4 * 2**20),
+    )(*results)
 
 
 def solution(mesh):

time: 37.2 us -> 31.7 us (0.85)
  local copies, waits for them, and re-layouts: 3.34 us -> 0 us
  Pallas kernels: 32.3 us -> 30.3 us
    unnamed x2 -> x0, local copies, waits for them, and re-layouts: 3.34 us -> none
    pallas_call x1 -> x2, Pallas kernels: 32.3 us -> 30.3 us  [the longest x1 29.4 us: on_device(): pl.pallas_call(functools.partial(kernel, patches), out_shape=(vmem((half,...]
where the time goes in v2:
time: 31.7 us; the launch traced here: 31.5 us
  Pallas kernels  30.3 us (96%)
  between operations  1.29 us (4%)
    pallas_call x1, Pallas kernels, on_device(): pl.pallas_call(functools.partial(kernel, patches), out_shape=(vmem((half,...  29.4 us
    pallas_call x1, Pallas kernels, on_device(): pl.pallas_call(put, out_shape=(jax.ShapeDtypeStruct((half, rows), bf16),...  0.82 us

profile of v2, /device:TPU:0, one launch (start us, length us, event | category | flops | bytes accessed | tf_op | source)
XLA Modules:
  0.0 31.5 jit_solution(2216817427533531257)
XLA Ops:
  1.3 29.4 %shard_map.176 = (bf16[256,128]{1,0:T(8,128)(2,1)S(1)}, bf16[256,1024]{1,0:T(8,128)(2,1)S(1)}) custom-call(bf16[256,128]{1,0:T(8,128)(2,1)} %nodes_in.1, bf16[256,1024]{1,0:T(8,128)(2,1)} %edges_in.1, s32[1,1024]{1,0:T(1,128)} %bitcast.2, s32[1,1024]{1,0:T(1,128)} %bitcast.3, s32[1]{0:T(128)S(6)} %copy.19.count_in, bf16[2,256,1536]{2,1,0:T(8,128)(2,1)} %wi_in.1, ...), custom_call_target="tpu_custom_call" | custom-call | tf_op jit(solution)/shard_map/pallas_call | solution.py:401
  30.7 0.8 %shard_map.177 = (bf16[256,128]{1,0:T(8,128)(2,1)}, bf16[256,1024]{1,0:T(8,128)(2,1)}) custom-call(bf16[256,128]{1,0:T(8,128)(2,1)S(1)} %get-tuple-element.4.nodes, bf16[256,1024]{1,0:T(8,128)(2,1)S(1)} %get-tuple-element.5.edges), custom_call_target="tpu_custom_call" | custom-call | tf_op jit(solution)/shard_map/pallas_call | solution.py:468

commit v3 on v2

--- a/solution.py
+++ b/solution.py
@@ -345,15 +345,13 @@
         ).astype(bf16)
         waited_out += [all_coarse] + relays + [swap]
 
-    store = pltpu.make_async_copy(nodes.at[here], nodes_out, out_sems.at[3])
-    store.start()
+    nodes_out[...] = nodes[here, :]
     for copy in remotes + waited_out:
         copy.wait_send()
     keep.wait()
     give.wait_send()
     got = edges_out.at[:, other_slots]
     remote(got, got, out_sems.at[1], out_sems.at[2], me, other).wait_recv()
-    store.wait()
 
 
 def put(nodes, edges, nodes_out, edges_out, sems):
@@ -443,7 +441,7 @@
             dma((layers, 3)),
             dma((layers, 3)),
             dma((layers, 2)),
-            dma((4,)),
+            dma((3,)),
         ],
         compiler_params=pltpu.CompilerParams(collective_id=0, has_side_effects=True, vmem_limit_bytes=56 * 2**20),
     )(

time: 31.7 us -> 31.6 us (level)
  no operation moved by 1% of the time
where the time goes in v3:
time: 31.6 us; the launch traced here: 31.4 us
  Pallas kernels  30.2 us (96%)
  between operations  1.29 us (4%)
    pallas_call x1, Pallas kernels, on_device(): pl.pallas_call(functools.partial(kernel, patches), out_shape=(vmem((half,...  29.3 us
    pallas_call x1, Pallas kernels, on_device(): pl.pallas_call(put, out_shape=(jax.ShapeDtypeStruct((half, rows), bf16),...  0.82 us

profile of v3, /device:TPU:0, one launch (start us, length us, event | category | flops | bytes accessed | tf_op | source)
XLA Modules:
  0.0 31.4 jit_solution(10473374017637092314)
XLA Ops:
  1.3 29.3 %shard_map.176 = (bf16[256,128]{1,0:T(8,128)(2,1)S(1)}, bf16[256,1024]{1,0:T(8,128)(2,1)S(1)}) custom-call(bf16[256,128]{1,0:T(8,128)(2,1)} %nodes_in.1, bf16[256,1024]{1,0:T(8,128)(2,1)} %edges_in.1, s32[1,1024]{1,0:T(1,128)} %bitcast.2, s32[1,1024]{1,0:T(1,128)} %bitcast.3, s32[1]{0:T(128)S(6)} %copy.19.count_in, bf16[2,256,1536]{2,1,0:T(8,128)(2,1)} %wi_in.1, ...), custom_call_target="tpu_custom_call" | custom-call | tf_op jit(solution)/shard_map/pallas_call | solution.py:399
  30.6 0.8 %shard_map.177 = (bf16[256,128]{1,0:T(8,128)(2,1)}, bf16[256,1024]{1,0:T(8,128)(2,1)}) custom-call(bf16[256,128]{1,0:T(8,128)(2,1)S(1)} %get-tuple-element.4.nodes, bf16[256,1024]{1,0:T(8,128)(2,1)S(1)} %get-tuple-element.5.edges), custom_call_target="tpu_custom_call" | custom-call | tf_op jit(solution)/shard_map/pallas_call | solution.py:466
